TPU v7x, 128 devices: a whole 4x4x4 slice. The times are simulated.
128 devices in a mesh: vp: 128 (over z, y, x, core).
Axes of the slice: x: 4, y: 4, z: 4, core: 2. Of those that a mesh axis runs over, the one named last changes fastest.
Arguments:
- residual: bfloat16 [16384, 2048], replicated
- labels: int32 [16384], replicated
- loss_mask: float32 [16384], replicated
- norm_gain: float32 [2048], replicated
- embed_table: bfloat16 [49408, 2048], P('vp')
Outputs:
- output 1: float32 [], replicated
- output 2: float32 [16384, 2048], P('vp')
- output 3: float32 [49408, 2048], P('vp')
- output 4: float32 [2048], replicated
All inputs are finite; a program needn't handle non-finite values.
Results may differ from a plain program's by a relative error of at most 0.001.
Values sent between devices are 32-bit elements.
A program may use at most 1 GiB of HBM per device.

v0:
```python
import jax
import jax.numpy as jnp
from jax import lax
from jax.sharding import PartitionSpec as P

VOCAB_REAL = 49155
LOGIT_SCALE = 6.0
NORM_EPS = 1e-6


def solution(mesh):
    vp_axis = mesh.axis_names[0]
    group_size = mesh.shape[vp_axis]

    def local_step(residual, labels, loss_mask, norm_gain, table_shard):
        tokens = residual.shape[0]
        shard_rows = table_shard.shape[0]
        tok_rows = tokens // group_size
        my_index = lax.axis_index(vp_axis)
        x_f32 = residual.astype(jnp.float32)
        inv_rms = lax.rsqrt(jnp.mean(x_f32 * x_f32, axis=-1, keepdims=True) + NORM_EPS)
        x_hat = x_f32 * inv_rms
        hidden = (x_hat * norm_gain).astype(jnp.bfloat16)
        logits = jnp.einsum('td,vd->tv', hidden, table_shard, preferred_element_type=jnp.float32) / LOGIT_SCALE
        col_ids = my_index * shard_rows + lax.broadcasted_iota(jnp.int32, (1, shard_rows), 1)
        logits = jnp.where(col_ids < VOCAB_REAL, logits, -jnp.inf)
        row_max = lax.pmax(jnp.max(logits, axis=-1), vp_axis)
        shifted = jnp.exp(logits - row_max[:, None])
        is_label = col_ids == labels[:, None]
        part_stats = jnp.stack([jnp.sum(shifted, axis=-1), jnp.sum(jnp.where(is_label, logits, 0.0), axis=-1)])
        row_stats = lax.psum(part_stats, vp_axis)
        sum_exp = row_stats[0]
        log_norm = row_max + jnp.log(sum_exp)
        mask_total = jnp.sum(loss_mask)
        tok_weight = loss_mask / mask_total
        mean_loss = jnp.sum(loss_mask * (log_norm - row_stats[1])) / mask_total
        row_prob = shifted / sum_exp[:, None]
        d_logits = (jnp.where(is_label, row_prob - 1.0, row_prob) * tok_weight[:, None]).astype(jnp.bfloat16)
        d_part = jnp.dot(d_logits, table_shard, preferred_element_type=jnp.float32) / LOGIT_SCALE
        d_embed = jnp.einsum('tv,td->vd', d_logits, hidden, preferred_element_type=jnp.float32) / LOGIT_SCALE
        d_hidden = lax.psum_scatter(d_part, vp_axis, scatter_dimension=0, tiled=True)
        x_hat_loc = lax.dynamic_slice_in_dim(x_hat, my_index * tok_rows, tok_rows, axis=0)
        inv_loc = lax.dynamic_slice_in_dim(inv_rms, my_index * tok_rows, tok_rows, axis=0)
        d_gain = lax.psum(jnp.sum(d_hidden * x_hat_loc, axis=0), vp_axis)
        value_a6 = d_hidden * norm_gain
        d_residual = inv_loc * (value_a6 - x_hat_loc * jnp.mean(value_a6 * x_hat_loc, axis=-1, keepdims=True))
        return mean_loss, d_residual, d_embed, d_gain

    return jax.shard_map(local_step, mesh=mesh, in_specs=(P(), P(), P(), P(), P(vp_axis, None)), out_specs=(P(), P(vp_axis, None), P(vp_axis, None), P()), check_vma=False)
```

profile of v0, /device:TPU:1, one launch (start us, length us, event | category | flops | bytes accessed | tf_op | source)
XLA Modules:
  0.0 1375.0 jit_solution(748975453481349570)
XLA Ops:
  7.2 0.0 copy-start
  7.2 0.0 all-reduce.4.cloned.1.call-start
  7.2 0.0 copy-start.4
  7.2 21.0 %fusion = f32[16384]{0:T(1024)S(1)} fusion(bf16[16384,2048]{1,0:T(8,128)(2,1)} %param.5), kind=kLoop, calls=%fused_computation.2 | loop fusion | flops 100646912 | bytes 67174400 | tf_op jit(solution)/shard_map/reduce_sum | solution.py:21
  28.3 0.0 copy-done
  28.3 0.0 copy-done.4
  28.3 0.0 copy-start.3
  28.3 40.6 %fusion.12 = (f32[16384]{0:T(1024)}, f32[16384,386]{0,1:T(8,128)}) fusion(bf16[386,2048]{1,0:T(8,128)(2,1)S(1)} %copy-done, f32[2048]{0:T(1024)S(1)} %copy-done.4, f32[16384]{0:T(1024)S(1)} %add_rsqrt_fusion, bf16[16384,2048]{1,0:T(8,128)(2,1)} %param.5, pred[386]{0:T(512)(128)(4,1)S(1)} %broadcast_compare_fusion), kind=kOutput, calls=%fused_computation.28 | convolution fusion | flops 26057195520 | bytes 94126464 | tf_op jit(solution)/shard_map/td,vd->tv/dot_general | solution.py:24
  68.9 0.0 all-reduce.4.cloned.1.call-update
  68.9 0.0 all-reduce.6.cloned.1.call-start
  69.0 149.0 %all-reduce.4.cloned.1.call-done = f32[16384]{0:T(1024)} async-done(((f32[16384]{0:T(1024)}), f32[16384]{0:T(1024)}) %all-reduce.4.cloned.1.call-update) | async-done | bytes 65552 | tf_op jit(solution)/shard_map/pmax | solution.py:27
  218.0 13.5 fusion.6
  231.5 0.8 pad_maximum_fusion
  232.3 0.0 all-reduce.6.cloned.1.call-update
  232.3 0.2 reduce-scatter.5.cloned.1.call-start
  232.5 144.7 %all-reduce.6.cloned.1.call-done = f32[2,16384]{1,0:T(2,128)} async-done(((f32[2,16384]{1,0:T(2,128)}), f32[2,16384]{1,0:T(2,128)}) %all-reduce.6.cloned.1.call-update) | async-done | bytes 131088 | tf_op jit(solution)/shard_map/psum | solution.py:31
  377.2 1.1 fusion.11
  378.3 0.0 copy-done.2
  378.3 0.0 copy-done.1
  378.3 0.6 fusion.10
  379.0 0.7 broadcast_divide_fusion
  379.6 58.7 %broadcast_multiply_fusion = f32[16384,2048]{1,0:T(8,128)} fusion(bf16[386,2048]{1,0:T(8,128)(2,1)S(1)} %copy-done, f32[16384,386]{0,1:T(8,128)} %get-tuple-element.13, f32[16384]{0:T(1024)S(1)} %broadcast_divide_fusion, f32[16384]{0:T(1024)S(1)} %bitcast.10, s32[16384]{0:T(1024)S(1)} %copy-done.3, f32[16384]{0:T(1024)S(1)} %copy-done.1, ...), kind=kOutput, calls=%fused_computation.4 | convolution fusion | flops 25981845504 | bytes 161359360 | tf_op jit(solution)/shard_map/dot_general | solution.py:39
  438.3 0.0 reduce-scatter.5.cloned.1.call-update
  438.3 0.6 dynamic-slice.3
  438.9 66.2 %convert_multiply_fusion = f32[16384,2048]{1,0:T(8,128)} fusion(bf16[16384,2048]{1,0:T(8,128)(2,1)} %param.5, f32[16384]{0:T(1024)S(1)} %add_rsqrt_fusion), kind=kLoop, calls=%fused_computation | loop fusion | flops 67108864 | bytes 201392128 | tf_op jit(solution)/shard_map/mul | solution.py:22
  506.4 0.0 copy-done.5
  506.4 0.0 copy-start.6
  506.5 41.1 %fusion.7 = f32[386,2048]{1,0:T(8,128)} fusion(f32[2048]{0:T(1024)S(1)} %copy-done.5, bf16[16384,2048]{1,0:T(8,128)(2,1)} %param.5, f32[16384]{0:T(1024)S(1)} %add_rsqrt_fusion, f32[16384,386]{0,1:T(8,128)} %get-tuple-element.13, f32[16384]{0:T(1024)S(1)} %broadcast_divide_fusion, f32[16384]{0:T(1024)S(1)} %bitcast.11, s32[16384]{0:T(1024)S(1)} %copy-done.3, ...), kind=kOutput, calls=%fused_computation.15 | convolution fusion | flops 26083299328 | bytes 95905288 | tf_op jit(solution)/shard_map/tv,td->vd/dot_general | solution.py:40
  547.6 747.1 %reduce-scatter.5.cloned.1.call-done = f32[128,2048]{1,0:T(8,128)} async-done(((f32[16384,2048]{1,0:T(8,128)}), f32[128,2048]{1,0:T(8,128)}) %reduce-scatter.5.cloned.1.call-update) | async-done | bytes 1048592
  1294.6 1.8 multiply_reduce_fusion
  1296.4 68.2 %psum.15 = f32[2048]{0:T(1024)} all-reduce(f32[2048]{0:T(1024)S(1)} %get-tuple-element.4), channel_id=1, replica_groups=mesh['vp'=128] {'vp'}, use_global_device_ids=true, to_apply=%region_11.12 | all-reduce | flops 2048 | bytes 16384 | tf_op jit(solution)/shard_map/psum | solution.py:44
  1364.6 2.7 subtract_multiply_fusion
  (9 shorter events, 0.0 us)
Async XLA Ops:
  7.2 21.1 %copy-start = (bf16[386,2048]{1,0:T(8,128)(2,1)S(1)}, bf16[386,2048]{1,0:T(8,128)(2,1)}, u32[]{:S(2)}) copy-start(bf16[386,2048]{1,0:T(8,128)(2,1)} %param.9) | copy-start | bytes 4743172
  7.2 210.8 %all-reduce.4.cloned.1.call-start = ((), (), s32[]{:S(2)}) async-start(), calls=%async_computation.1 | async-start | bytes 131072 | tf_op jit(solution)/shard_map/pmax | solution.py:27
  7.2 21.1 %copy-start.4 = (f32[2048]{0:T(1024)S(1)}, f32[2048]{0:T(1024)}, u32[]{:S(2)}) copy-start(f32[2048]{0:T(1024)} %param.8) | copy-start | bytes 24580
  28.3 189.7 %copy-start.3 = (s32[16384]{0:T(1024)S(1)}, s32[16384]{0:T(1024)}, u32[]{:S(2)}) copy-start(s32[16384]{0:T(1024)} %param.6) | copy-start | bytes 196612
  68.9 309.4 %copy-start.2 = (f32[16384]{0:T(1024)S(1)}, f32[16384]{0:T(1024)}, u32[]{:S(2)}) copy-start(f32[16384]{0:T(1024)} %param.7) | copy-start | bytes 196612
  68.9 308.3 %all-reduce.6.cloned.1.call-start = ((), (), s32[]{:S(2)}) async-start(), calls=%async_computation.2 | async-start | bytes 262144 | tf_op jit(solution)/shard_map/psum | solution.py:31
  218.0 160.3 %copy-start.1 = (f32[16384]{0:T(1024)S(1)}, f32[16384]{0:T(1024)}, u32[]{:S(2)}) copy-start(f32[16384]{0:T(1024)} %all-reduce.4.cloned.1.call-done) | copy-start | bytes 196612
  232.3 1062.3 %reduce-scatter.5.cloned.1.call-start = ((), (), s32[]{:S(2)}) async-start(), calls=%async_computation.3 | async-start | bytes 135266304
  438.9 67.5 %copy-start.5 = (f32[2048]{0:T(1024)S(1)}, f32[2048]{0:T(1024)}, u32[]{:S(2)}) copy-start(f32[2048]{0:T(1024)} %param.8) | copy-start | bytes 24580
  506.4 858.1 %copy-start.6 = (f32[128]{0:T(128)S(1)}, f32[128]{0:T(128)}, u32[]{:S(2)}) copy-start(f32[128]{0:T(128)} %dynamic-slice.3) | copy-start | bytes 1540
Sparse Core Ops, SparseCore 0:
  69.0 148.9 all-reduce.3
  232.4 144.7 all-reduce.5
  438.5 856.1 reduce-scatter.4
where the time goes:
time: 1380 us
  waiting for transfers between devices  1040 us (75%)
  matrix products  140 us (10%)
  other arithmetic  107 us (8%)
  blocking collectives  68.2 us (5%)
  between operations  16.3 us (1%)
    unnamed x4, waiting for transfers between devices  747 us
    pmax x1, waiting for transfers between devices, local_step(): row_max = lax.pmax(jnp.max(logits, axis=-1), vp_axis)  149 us
    psum x1, waiting for transfers between devices, local_step(): row_stats = lax.psum(part_stats, vp_axis)  145 us
    psum x1, blocking collectives, local_step(): d_gain = lax.psum(jnp.sum(d_hidden * x_hat_loc, axis=0), vp_axis)  68.2 us
    mul x1, other arithmetic, local_step(): x_hat = x_f32 * inv_rms  66.2 us
    dot_general x1, matrix products, local_step(): jnp.dot(d_logits, table_shard, preferred_element_type=jnp.float32)  58.7 us
    dot_general x1, matrix products, local_step(): jnp.einsum('tv,td->vd', d_logits, hidden, preferred_element_type=jnp.floa...  41.1 us
    dot_general x1, matrix products, local_step(): jnp.einsum('td,vd->tv', hidden, table_shard, preferred_element_type=jnp.f...  40.6 us
  transfers between devices with their start and end apart: 3, of which 3 were waited for; matrix products, arithmetic and copies ran while one was open for 8% of the time, Pallas kernels for 0%

commit v1 on v0

v1 whole, which is shorter than its diff:
```python
import functools

import jax
import jax.numpy as jnp
from jax import lax
from jax.experimental import pallas as pl
from jax.experimental.pallas import tpu as pltpu
from jax.sharding import PartitionSpec as P

VOCAB_REAL = 49155
LOGIT_SCALE = 6.0
NORM_EPS = 1e-6

AXIS = "vp"
MESH = pl.DeviceIdType.MESH
F32 = jnp.float32
BF16 = jnp.bfloat16
HBM = pltpu.HBM
VMEM = pltpu.VMEM
DMA = pltpu.SemaphoreType.DMA


def _coords():
    me = lax.axis_index(AXIS)
    return me // 32, (me // 8) % 4, (me // 2) % 4, me % 2


def _dev(z, y, x, c):
    return ((z * 4 + y) * 4 + x) * 2 + c


def _mod4(v):
    return lax.rem(v + 8, 4)


def _barrier(peers):
    sem = pltpu.get_barrier_semaphore()
    for p in peers:
        pl.semaphore_signal(sem, inc=1, device_id=(p,), device_id_type=MESH)
    pl.semaphore_wait(sem, len(peers))


def _remote(src, dst, send, recv, k, dev):
    return pltpu.make_async_remote_copy(
        src_ref=src,
        dst_ref=dst,
        send_sem=send.at[k],
        recv_sem=recv.at[k],
        device_id=(dev,),
        device_id_type=MESH,
    )


def _gather_kernel(ra, e_ref, out_ref, tmp, send, recv, lsem):
    z, y, x, c = _coords()
    rows = e_ref.shape[0]
    right, left = _dev(z, y, _mod4(x + 1), c), _dev(z, y, _mod4(x - 1), c)
    sib = _dev(z, y, x, 1 - c)
    _barrier((right, left, sib))
    a, b = pl.ds(0, ra), pl.ds(ra, rows - ra)

    def slot(xx):
        return _mod4(xx) * 2 + c

    own = slot(x)
    cp_in = pltpu.make_async_copy(e_ref, tmp, lsem.at[0])
    cp_in.start()
    r_a = _remote(e_ref.at[a], out_ref.at[own, a], send, recv, 0, right)
    r_b = _remote(e_ref.at[b], out_ref.at[own, b], send, recv, 1, right)
    l_b = _remote(e_ref.at[b], out_ref.at[own, b], send, recv, 2, left)
    l_a = _remote(e_ref.at[a], out_ref.at[own, a], send, recv, 3, left)
    s_o = _remote(e_ref, out_ref.at[own], send, recv, 6, sib)
    for cp in (r_a, l_b, r_b, l_a, s_o):
        cp.start()
    cp_in.wait()
    cp_out = pltpu.make_async_copy(tmp, out_ref.at[own], lsem.at[1])
    cp_out.start()

    def fwd(s, half, k, dev):
        ref = out_ref.at[s, half]
        return _remote(ref, ref, send, recv, k, dev)

    sl, sr, sf = slot(x - 1), slot(x + 1), slot(x + 2)
    later = []
    r_a.wait_recv()
    r_f = fwd(sl, a, 4, right)
    r_f.start()
    later.append(fwd(sl, a, 7, sib))
    later[-1].start()
    l_b.wait_recv()
    l_f = fwd(sr, b, 5, left)
    l_f.start()
    later.append(fwd(sr, b, 8, sib))
    later[-1].start()
    r_b.wait_recv()
    later.append(fwd(sl, b, 9, sib))
    later[-1].start()
    l_a.wait_recv()
    later.append(fwd(sr, a, 10, sib))
    later[-1].start()
    r_f.wait_recv()
    later.append(fwd(sf, a, 11, sib))
    later[-1].start()
    l_f.wait_recv()
    later.append(fwd(sf, b, 12, sib))
    later[-1].start()
    cp_out.wait()
    s_o.wait_recv()
    for cp in later:
        cp.wait_recv()
    for cp in (r_a, r_b, l_b, l_a, s_o, r_f, l_f, *later):
        cp.wait_send()


def _gather(e32, ra):
    rows, d = e32.shape
    return pl.pallas_call(
        functools.partial(_gather_kernel, ra),
        name="table_gather",
        out_shape=jax.ShapeDtypeStruct((8, rows, d), F32),
        in_specs=[pl.BlockSpec(memory_space=HBM)],
        out_specs=pl.BlockSpec(memory_space=HBM),
        scratch_shapes=[VMEM((rows, d), F32), DMA((13,)), DMA((13,)), DMA((2,))],
        compiler_params=pltpu.CompilerParams(
            collective_id=0, has_side_effects=True, vmem_limit_bytes=60 << 20
        ),
    )(e32)


def _stats_kernel(st_ref, lse_ref, tgt_ref, got, send, recv):
    z, y, x, c = _coords()
    peers = [
        (_mod4(z + dz), _mod4(y + dy)) for dz in range(4) for dy in range(4) if dz or dy
    ]
    ids = [_dev(pz, py, x, c) for pz, py in peers]
    _barrier(ids)
    cps = []
    for k, dev in enumerate(ids):
        cp = _remote(st_ref, got.at[k], send, recv, k, dev)
        cp.start()
        cps.append(cp)
    n = lse_ref.shape[0]
    m, s, t = st_ref[0:n], st_ref[n : 2 * n], st_ref[2 * n : 3 * n]
    for cp in cps:
        cp.wait_recv()
    top = m
    for k in range(15):
        top = jnp.maximum(top, got[k, 0:n])
    s = s * jnp.exp(m - top)
    for k in range(15):
        s = s + got[k, n : 2 * n] * jnp.exp(got[k, 0:n] - top)
        t = t + got[k, 2 * n : 3 * n]
    lse_ref[...] = top + jnp.log(s)
    tgt_ref[...] = t
    for cp in cps:
        cp.wait_send()


def _stats(st):
    n = st.shape[0] // 3
    vm = pl.BlockSpec(memory_space=VMEM)
    one = jax.ShapeDtypeStruct((n, 128), F32)
    return pl.pallas_call(
        _stats_kernel,
        name="row_stats",
        out_shape=(one, one),
        in_specs=[vm],
        out_specs=(vm, vm),
        scratch_shapes=[VMEM((15, 3 * n, 128), F32), DMA((15,)), DMA((15,))],
        compiler_params=pltpu.CompilerParams(collective_id=1, has_side_effects=True),
    )(st)


def _add_rows(dst, srcs, step):
    rows = dst.shape[0]

    @pl.loop(0, rows // step)
    def _(i):
        r = pl.ds(pl.multiple_of(i * step, step), step)
        acc = dst[r, :]
        for s in srcs:
            acc = acc + s[r, :]
        dst[r, :] = acc


def _reduce_kernel(
    dh_ref, de_ref, dh_out, de_out,
    q, s, xa, xb, xl, xr,
    acc_r, acc_l, own, ya, yb, yl, yr, za, zb, zl, zr,
    send_e, recv_e, send_h, recv_h, lsem,
):
    z, y, x, c = _coords()
    half = dh_ref.shape[-1] // 2
    chunk = dh_ref.shape[2]
    hc = chunk // 2
    xp, xm = _dev(z, y, _mod4(x + 1), c), _dev(z, y, _mod4(x - 1), c)
    yp, ym = _dev(z, _mod4(y + 1), x, c), _dev(z, _mod4(y - 1), x, c)
    zp, zm = _dev(_mod4(z + 1), y, x, c), _dev(_mod4(z - 1), y, x, c)
    sib = _dev(z, y, x, 1 - c)
    _barrier((xp, xm, yp, ym, zp, zm, sib))

    order = (_mod4(x + 2), _mod4(x + 1), _mod4(x - 1), x)
    cols = (pl.ds(0, half), pl.ds(half, half))
    ring1, ring2 = ((yp, ym), (zp, zm)), ((zp, zm), (yp, ym))
    pos1, pos2 = (y, z), (z, y)

    def part(k, p, lo, n):
        if k == 0:
            return dh_ref.at[pl.ds(lo, n), p, :, cols[0]]
        return dh_ref.at[p, pl.ds(lo, n), :, cols[1]]

    loads = []
    d2d = []
    for i in range(4):
        cp = _remote(de_ref.at[order[i] * 2 + 1 - c], s.at[i], send_e, recv_e, i, sib)
        cp.start()
        d2d.append(cp)
        ld = pltpu.make_async_copy(de_ref.at[order[i] * 2 + c], q.at[i], lsem.at[i])
        ld.start()
        loads.append(ld)
    first = []
    for k in range(2):
        p = pos1[k]
        rt, lt = ring1[k]
        cps = [
            _remote(part(k, _mod4(p + 2), 0, 2), ya.at[k], send_h, recv_h, (k, 0), rt),
            _remote(part(k, _mod4(p + 2), 2, 2), yb.at[k], send_h, recv_h, (k, 1), lt),
            _remote(part(k, _mod4(p + 1), 2, 2), yl.at[k, pl.ds(2, 2)], send_h, recv_h, (k, 2), rt),
            _remote(part(k, _mod4(p - 1), 0, 2), yr.at[k, pl.ds(0, 2)], send_h, recv_h, (k, 3), lt),
        ]
        for cp in cps:
            cp.start()
        first.append(cps)
        lds = [
            pltpu.make_async_copy(part(k, _mod4(p + 1), 0, 2), acc_r.at[k], lsem.at[4 + 3 * k]),
            pltpu.make_async_copy(part(k, _mod4(p - 1), 2, 2), acc_l.at[k], lsem.at[5 + 3 * k]),
            pltpu.make_async_copy(part(k, p, 0, 4), own.at[k], lsem.at[6 + 3 * k]),
        ]
        for ld in lds:
            ld.start()
        loads += lds

    sent = list(d2d) + first[0] + first[1]

    def go(cp):
        cp.start()
        sent.append(cp)
        return cp

    for i in range(4):
        loads[i].wait()
        d2d[i].wait_recv()
        _add_rows(q.at[i], [s.at[i]], 8)
        if i == 0:
            e0 = go(_remote(q.at[0, :, cols[0]], xa, send_e, recv_e, 4, xp))
            e1 = go(_remote(q.at[0, :, cols[1]], xb, send_e, recv_e, 5, xm))
        if i == 1:
            e2 = go(_remote(q.at[1, :, cols[1]], xl.at[:, cols[1]], send_e, recv_e, 6, xp))
        if i == 2:
            e3 = go(_remote(q.at[2, :, cols[0]], xr.at[:, cols[0]], send_e, recv_e, 7, xm))

    for k in range(2):
        rt, lt = ring1[k]
        loads[4 + 3 * k].wait()
        first[k][0].wait_recv()
        for i in range(2):
            _add_rows(acc_r.at[k, i], [ya.at[k, i]], 8)
        first[k].append(go(_remote(acc_r.at[k], yl.at[k, pl.ds(0, 2)], send_h, recv_h, (k, 4), rt)))
        loads[5 + 3 * k].wait()
        first[k][1].wait_recv()
        for i in range(2):
            _add_rows(acc_l.at[k, i], [yb.at[k, i]], 8)
        first[k].append(go(_remote(acc_l.at[k], yr.at[k, pl.ds(2, 2)], send_h, recv_h, (k, 5), lt)))

    e0.wait_recv()
    _add_rows(q.at[1, :, cols[0]], [xa], 8)
    e4 = go(_remote(q.at[1, :, cols[0]], xl.at[:, cols[0]], send_e, recv_e, 8, xp))
    e1.wait_recv()
    _add_rows(q.at[2, :, cols[1]], [xb], 8)
    e5 = go(_remote(q.at[2, :, cols[1]], xr.at[:, cols[1]], send_e, recv_e, 9, xm))

    lo, hi = pl.ds(0, hc), pl.ds(hc, hc)
    second = []
    for k in range(2):
        loads[6 + 3 * k].wait()
        for cp in first[k][2:]:
            cp.wait_recv()
        for i in range(4):
            _add_rows(own.at[k, i], [yl.at[k, i], yr.at[k, i]], 8)
        r = pos2[k]
        rt, lt = ring2[k]
        second.append([
            go(_remote(own.at[k, _mod4(r + 2), lo], za.at[k], send_h, recv_h, (k, 6), rt)),
            go(_remote(own.at[k, _mod4(r + 2), hi], zb.at[k], send_h, recv_h, (k, 7), lt)),
            go(_remote(own.at[k, _mod4(r + 1), hi], zl.at[k, hi], send_h, recv_h, (k, 8), rt)),
            go(_remote(own.at[k, _mod4(r - 1), lo], zr.at[k, lo], send_h, recv_h, (k, 9), lt)),
        ])
    for k in range(2):
        r = pos2[k]
        rt, lt = ring2[k]
        second[k][0].wait_recv()
        _add_rows(own.at[k, _mod4(r + 1), lo], [za.at[k]], 8)
        second[k].append(go(_remote(own.at[k, _mod4(r + 1), lo], zl.at[k, lo], send_h, recv_h, (k, 10), rt)))
        second[k][1].wait_recv()
        _add_rows(own.at[k, _mod4(r - 1), hi], [zb.at[k]], 8)
        second[k].append(go(_remote(own.at[k, _mod4(r - 1), hi], zr.at[k, hi], send_h, recv_h, (k, 11), lt)))
    outs = []
    for k in range(2):
        r = pos2[k]
        for cp in second[k][2:]:
            cp.wait_recv()
        _add_rows(own.at[k, r], [zl.at[k], zr.at[k]], 8)
        cp = pltpu.make_async_copy(own.at[k, r], dh_out.at[:, cols[k]], lsem.at[10 + k])
        cp.start()
        outs.append(cp)

    for cp in (e2, e3, e4, e5):
        cp.wait_recv()
    _add_rows(q.at[3], [xl, xr], 8)
    cp = pltpu.make_async_copy(q.at[3], de_out, lsem.at[12])
    cp.start()
    outs.append(cp)
    for cp in outs:
        cp.wait()
    for cp in sent:
        cp.wait_send()


def _reduce(dh, de):
    _, _, chunk, d = dh.shape
    _, rows, _ = de.shape
    h, hc = d // 2, chunk // 2
    hbm = pl.BlockSpec(memory_space=HBM)
    return pl.pallas_call(
        _reduce_kernel,
        name="grad_reduce",
        out_shape=(jax.ShapeDtypeStruct((chunk, d), F32), jax.ShapeDtypeStruct((rows, d), F32)),
        in_specs=[hbm, hbm],
        out_specs=(hbm, hbm),
        scratch_shapes=[
            VMEM((4, rows, d), F32), VMEM((4, rows, d), F32),
            VMEM((rows, h), F32), VMEM((rows, h), F32), VMEM((rows, d), F32), VMEM((rows, d), F32),
            VMEM((2, 2, chunk, h), F32), VMEM((2, 2, chunk, h), F32), VMEM((2, 4, chunk, h), F32),
            VMEM((2, 2, chunk, h), F32), VMEM((2, 2, chunk, h), F32),
            VMEM((2, 4, chunk, h), F32), VMEM((2, 4, chunk, h), F32),
            VMEM((2, hc, h), F32), VMEM((2, hc, h), F32), VMEM((2, chunk, h), F32), VMEM((2, chunk, h), F32),
            DMA((10,)), DMA((10,)), DMA((2, 12)), DMA((2, 12)), DMA((13,)),
        ],
        compiler_params=pltpu.CompilerParams(
            collective_id=2, has_side_effects=True, vmem_limit_bytes=67043328
        ),
    )(dh, de)


def _allsum_kernel(v_ref, o_ref, mid, got1, got2, send1, recv1, send2, recv2):
    z, y, x, c = _coords()
    near = [_dev(_mod4(z + a), _mod4(y + b), x, c) for a in range(4) for b in range(4) if a or b]
    far = [_dev(z, y, _mod4(x + a), lax.rem(c + b, 2)) for a in range(4) for b in range(2) if a or b]
    _barrier(near + far)
    cps = [_remote(v_ref, got1.at[k], send1, recv1, k, dev) for k, dev in enumerate(near)]
    for cp in cps:
        cp.start()
    for cp in cps:
        cp.wait_recv()
    tot = v_ref[...]
    for k in range(15):
        tot = tot + got1[k]
    mid[...] = tot
    cps2 = [_remote(mid, got2.at[k], send2, recv2, k, dev) for k, dev in enumerate(far)]
    for cp in cps2:
        cp.start()
    for cp in cps2:
        cp.wait_recv()
    tot = mid[...]
    for k in range(7):
        tot = tot + got2[k]
    o_ref[...] = tot
    for cp in cps + cps2:
        cp.wait_send()


def _allsum(v):
    vm = pl.BlockSpec(memory_space=VMEM)
    return pl.pallas_call(
        _allsum_kernel,
        name="small_sum",
        out_shape=jax.ShapeDtypeStruct(v.shape, F32),
        in_specs=[vm],
        out_specs=vm,
        scratch_shapes=[
            VMEM(v.shape, F32), VMEM((15, *v.shape), F32), VMEM((7, *v.shape), F32),
            DMA((15,)), DMA((15,)), DMA((7,)), DMA((7,)),
        ],
        compiler_params=pltpu.CompilerParams(collective_id=3, has_side_effects=True),
    )(v)


def solution(mesh):
    group = mesh.shape[AXIS]

    def local_step(residual, labels, loss_mask, norm_gain, table_shard):
        tokens, dim = residual.shape
        rows = table_shard.shape[0]
        chunk = tokens // group
        pad = -rows % 8 + rows
        me = lax.axis_index(AXIS)
        xc, zy = lax.rem(me, 8), me // 8
        tok = tokens // 8

        e32 = jnp.pad(table_shard.astype(F32), ((0, pad - rows), (0, 0)))
        ra = (pad // 2) // 8 * 8
        table = _gather(e32, ra).astype(BF16).reshape(8 * pad, dim)

        def mine(v):
            v = v.reshape(16, 8, chunk, *v.shape[1:])
            return lax.dynamic_index_in_dim(v, xc, 1, keepdims=False).reshape(tok, *v.shape[3:])

        x_f32 = mine(residual).astype(F32)
        lab = mine(labels)
        msk = mine(loss_mask)
        inv_rms = lax.rsqrt(jnp.mean(x_f32 * x_f32, axis=-1, keepdims=True) + NORM_EPS)
        hidden = (x_f32 * inv_rms * norm_gain).astype(BF16)
        mask_total = jnp.sum(loss_mask)

        row = lax.broadcasted_iota(jnp.int32, (8, pad), 1)
        col_ids = (zy * 8 + lax.broadcasted_iota(jnp.int32, (8, pad), 0)) * rows + row
        col_ids = jnp.where((row < rows) & (col_ids < VOCAB_REAL), col_ids, -1).reshape(1, 8 * pad)
        z = jnp.einsum('td,vd->tv', hidden, table, preferred_element_type=F32) / LOGIT_SCALE
        z = jnp.where(col_ids >= 0, z, -jnp.inf)
        is_label = col_ids == lab[:, None]
        top = jnp.max(z, axis=-1)
        part_sum = jnp.sum(jnp.exp(z - top[:, None]), axis=-1)
        part_tgt = jnp.sum(jnp.where(is_label, z, 0.0), axis=-1)
        st = jnp.concatenate([v.reshape(tok // 128, 128) for v in (top, part_sum, part_tgt)])
        lse, tgt = _stats(st)
        lse, tgt = lse.reshape(tok), tgt.reshape(tok)
        prob = jnp.exp(z - lse[:, None])
        dz = (jnp.where(is_label, prob - 1.0, prob) * (msk / mask_total)[:, None]).astype(BF16)
        dh_part = jnp.dot(dz, table, preferred_element_type=F32)
        de_part = jnp.einsum('tv,td->vd', dz, hidden, preferred_element_type=F32)
        dh, de = _reduce(dh_part.reshape(4, 4, chunk, dim), de_part.reshape(8, pad, dim))

        dh = dh / LOGIT_SCALE
        d_embed = de[:rows] / LOGIT_SCALE
        x_loc = lax.dynamic_slice_in_dim(residual, me * chunk, chunk, axis=0).astype(F32)
        inv_loc = lax.rsqrt(jnp.mean(x_loc * x_loc, axis=-1, keepdims=True) + NORM_EPS)
        x_hat = x_loc * inv_loc
        dg_part = jnp.sum(dh * x_hat, axis=0)
        loss_part = jnp.where(zy == 0, jnp.sum(msk * (lse - tgt)), 0.0)
        small = jnp.concatenate([dg_part, jnp.full((1024,), loss_part)]).reshape(-1, 128)
        small = _allsum(small).reshape(-1)
        u = dh * norm_gain
        d_res = inv_loc * (u - x_hat * jnp.mean(u * x_hat, axis=-1, keepdims=True))
        return small[dim] / mask_total, d_res, d_embed, small[:dim]

    return jax.shard_map(
        local_step,
        mesh=mesh,
        in_specs=(P(), P(), P(), P(), P(AXIS, None)),
        out_specs=(P(), P(AXIS, None), P(AXIS, None), P()),
        check_vma=False,
    )
```

time: 1380 us -> 482 us (0.35)
  waiting for transfers between devices: 1040 us -> 0 us
  Pallas kernels: 0 us -> 260 us
  blocking collectives: 68.2 us -> 0 us
  matrix products: 140 us -> 99.3 us
  local copies, waits for them, and re-layouts: 1.72 us -> 34 us
  other arithmetic: 107 us -> 83.2 us
    unnamed x4 -> x0, waiting for transfers between devices: 747 us -> none
    pallas_call x0 -> x4, Pallas kernels: none -> 260 us  [the longest x1 118 us: _reduce(): pl.pallas_call(_reduce_kernel, name='grad_reduce', out_shape=(jax.ShapeDt...]
    pmax x1 -> x0, waiting for transfers between devices: 149 us -> none  [local_step(): row_max = lax.pmax(jnp.max(logits, axis=-1), vp_axis)]
    psum x1 -> x0, waiting for transfers between devices: 145 us -> none  [local_step(): row_stats = lax.psum(part_stats, vp_axis)]
    psum x1 -> x0, blocking collectives: 68.2 us -> none  [local_step(): d_gain = lax.psum(jnp.sum(d_hidden * x_hat_loc, axis=0), vp_axis)]
    mul x2 -> x3, other arithmetic: 68.9 us -> 3.99 us  [the longest x1 2.69 us: local_step(): d_res = inv_loc * (u - x_hat * jnp.mean(u * x_hat, axis=-1, keepdims=True))]
    convert_element_type x0 -> x4, other arithmetic: none -> 46.9 us  [the longest x2 27.8 us: local_step(): (jnp.where(is_label, prob - 1.0, prob) * (msk / mask_total)[:, None]).ast...]
    dot_general x3, matrix products: 140 us -> 99.3 us  [the longest x1 36.4 us: local_step(): dh_part = jnp.dot(dz, table, preferred_element_type=F32)]
  transfers between devices with their start and end apart: 3 -> 0, of which waited for: 3 -> 0; matrix products, arithmetic and copies ran while one was open for 8% -> 0% of each run, Pallas kernels for 0% -> 0%
where the time goes in v1:
time: 482 us; the launch traced here: 481 us
  Pallas kernels  260 us (54%)
  matrix products  99.3 us (21%)
  other arithmetic  83.2 us (17%)
  local copies, waits for them, and re-layouts  34 us (7%)
    pallas_call x1, Pallas kernels, _reduce(): pl.pallas_call(_reduce_kernel, name='grad_reduce', out_shape=(jax.ShapeDt...  118 us
    pallas_call x1, Pallas kernels, _gather(): pl.pallas_call(functools.partial(_gather_kernel, ra), name='table_gather'...  114 us
    dot_general x1, matrix products, local_step(): dh_part = jnp.dot(dz, table, preferred_element_type=F32)  36.4 us
    dot_general x1, matrix products, local_step(): de_part = jnp.einsum('tv,td->vd', dz, hidden, preferred_element_type=F32)  32.3 us
    dot_general x1, matrix products, local_step(): jnp.einsum('td,vd->tv', hidden, table, preferred_element_type=F32)  30.6 us
    convert_element_type x2, other arithmetic, local_step(): (jnp.where(is_label, prob - 1.0, prob) * (msk / mask_total)[:, None]).ast...  27.8 us
    dot_general x1, local copies, waits for them, and re-layouts, local_step(): dh_part = jnp.dot(dz, table, preferred_element_type=F32)  27 us
    pallas_call x1, Pallas kernels, _allsum(): pl.pallas_call(_allsum_kernel, name='small_sum', out_shape=jax.ShapeDtype...  14.4 us

profile of v1, /device:TPU:1, one launch (start us, length us, event | category | flops | bytes accessed | tf_op | source)
XLA Modules:
  0.0 480.5 jit_solution(668673309518689933)
XLA Ops:
  0.7 1.5 reduce_sum.75
  2.1 1.2 fusion.17
  3.3 0.5 add_rsqrt_fusion.1
  3.9 0.1 iota.20
  4.0 1.3 broadcast_multiply_fusion
  5.3 0.8 constant_dynamic-slice_fusion.1
  6.2 0.8 constant_dynamic-slice_fusion
  7.0 5.1 %fusion.5 = f32[16,128]{1,0:T(8,128)S(1)} fusion(bf16[16,8,128,2048]{3,2,1,0:T(8,128)(2,1)} %bitcast.2, s32[]{:T(128)S(6)} %select_n.51), kind=kLoop, calls=%fused_computation.13 | loop fusion | flops 12580864 | bytes 8396804 | tf_op jit(solution)/shard_map/reduce_sum | solution.py:421
  12.3 3.5 pad_convert_fusion.e_ref
  15.8 8.6 %fusion.7 = bf16[16,1,128,2048]{3,2,1,0:T(8,128)(2,1)} fusion(f32[2048]{0:T(1024)} %param.8, f32[16,128]{1,0:T(8,128)S(1)} %add_rsqrt_fusion, bf16[16,8,128,2048]{3,2,1,0:T(8,128)(2,1)} %bitcast.2, s32[]{:T(128)S(6)} %select_n.51), kind=kLoop, calls=%fused_computation.15 | loop fusion | flops 16777216 | bytes 16793604 | tf_op jit(solution)/shard_map/convert_element_type | solution.py:422
  24.4 113.6 %table_gather.1 = f32[8,392,2048]{2,1,0:T(8,128)} custom-call(f32[392,2048]{1,0:T(8,128)} %pad_convert_fusion.e_ref), custom_call_target="tpu_custom_call" | custom-call | tf_op jit(solution)/shard_map/table_gather/pallas_call | solution.py:117
  138.0 10.5 %convert_element_type.31 = bf16[8,392,2048]{2,1,0:T(8,128)(2,1)S(1)} convert(f32[8,392,2048]{2,1,0:T(8,128)} %table_gather.1) | non-fusion elementwise | flops 6422528 | bytes 38535168 | tf_op jit(solution)/shard_map/convert_element_type | solution.py:412
  148.6 0.2 copy-done.2
  148.8 30.6 %fusion.19 = (f32[2048]{0:T(1024)S(1)}, f32[2048,3136]{0,1:T(8,128)}) fusion(bf16[2048,2048]{1,0:T(8,128)(2,1)S(1)} %bitcast.45, bf16[3136,2048]{1,0:T(8,128)(2,1)S(1)} %bitcast.39, pred[3136]{0:T(1024)(128)(4,1)S(1)} %get-tuple-element.16), kind=kOutput, calls=%fused_computation.47 | convolution fusion | flops 26325940224 | bytes 46935104 | tf_op jit(solution)/shard_map/td,vd->tv/dot_general | solution.py:428
  179.4 11.9 %exponential_reduce_fusion = (f32[2048]{0:T(1024)S(1)}, f32[2048]{0:T(1024)S(1)}) fusion(f32[2048,3136]{0,1:T(8,128)} %get-tuple-element.21, f32[2048]{0:T(1024)S(1)} %get-tuple-element.20, s32[2048]{0:T(1024)S(1)} %bitcast.46, s32[3136]{0:T(1024)S(1)} %get-tuple-element.17), kind=kLoop, calls=%fused_computation.9 | loop fusion | flops 32108544 | bytes 25735424 | tf_op jit(solution)/shard_map/reduce_sum | solution.py:432
  191.3 0.6 pad_maximum_fusion.st_ref
  191.9 14.2 %row_stats.1 = (f32[16,128]{1,0:T(8,128)}, f32[16,128]{1,0:T(8,128)}) custom-call(f32[48,128]{1,0:T(8,128)} %pad_maximum_fusion.st_ref), custom_call_target="tpu_custom_call" | custom-call | tf_op jit(solution)/shard_map/row_stats/pallas_call | solution.py:163
  206.2 2.0 fusion.18
  208.8 18.6 %fusion.2 = bf16[2048,3136]{0,1:T(8,128)(2,1)} fusion(f32[2048,3136]{0,1:T(8,128)} %get-tuple-element.21, f32[2048]{0:T(1024)S(1)} %get-tuple-element.19, f32[2048]{0:T(1024)} %bitcast.50, s32[2048]{0:T(1024)S(1)} %bitcast.47, s32[3136]{0:T(1024)S(1)} %get-tuple-element.17), kind=kLoop, calls=%fused_computation.5 | loop fusion | flops 38535168 | bytes 38572288 | tf_op jit(solution)/shard_map/convert_element_type | solution.py:438
  227.4 1.8 copy-done
  229.2 9.2 %fusion.4 = bf16[3136,2048]{1,0:T(8,128)(2,1)} fusion(f32[2048,3136]{0,1:T(8,128)S(1)} %copy-done, f32[2048]{0:T(1024)S(1)} %get-tuple-element.19, s32[2048]{0:T(1024)S(1)} %bitcast.48, f32[2048]{0:T(1024)S(1)} %bitcast.51, s32[3136]{0:T(1024)S(1)} %get-tuple-element.17), kind=kLoop, calls=%fused_computation.7 | loop fusion | flops 38535168 | bytes 38572288 | tf_op jit(solution)/shard_map/convert_element_type | solution.py:438
  238.4 27.0 %dot_general.14 = bf16[4,4,128,3136]{2,1,0,3:T(4,128)(2,1)} reshape(bf16[2048,3136]{0,1:T(8,128)(2,1)} %fusion.2) | data formatting | bytes 25690112 | tf_op jit(solution)/shard_map/dot_general | solution.py:439
  265.4 36.4 %fusion.8.dh_ref = f32[4,4,128,2048]{3,2,1,0:T(8,128)} fusion(bf16[3136,2048,1,1]{1,0,3,2:T(8,128)(2,1)} %bitcast.40, bf16[4,4,128,3136]{2,1,0,3:T(4,128)(2,1)} %dot_general.14), kind=kOutput, calls=%fused_computation.16 | convolution fusion | flops 26306674688 | bytes 42467328 | tf_op jit(solution)/shard_map/dot_general | solution.py:439
  301.8 32.3 %fusion.20.de_ref = f32[8,392,2048]{2,1,0:T(8,128)} fusion(bf16[8,392,2048]{2,1,0:T(8,128)(2,1)S(1)} %bitcast.43, bf16[2048,2048,1]{1,0,2:T(8,128)(2,1)} %bitcast.44), kind=kOutput, calls=%fused_computation.48 | convolution fusion | flops 26306674688 | bytes 46923776 | tf_op jit(solution)/shard_map/tv,td->vd/dot_general | solution.py:440
  334.1 117.9 %grad_reduce.1 = (f32[128,2048]{1,0:T(8,128)}, f32[392,2048]{1,0:T(8,128)}) custom-call(f32[4,4,128,2048]{3,2,1,0:T(8,128)} %fusion.8.dh_ref, f32[8,392,2048]{2,1,0:T(8,128)} %fusion.20.de_ref), custom_call_target="tpu_custom_call" | custom-call | tf_op jit(solution)/shard_map/grad_reduce/pallas_call | solution.py:334
  451.9 4.1 slice_multiply_fusion
  456.0 1.8 fusion.14
  457.8 2.7 fusion.16
  460.5 0.6 pad_bitcast_fusion.v_ref
  461.1 14.4 %small_sum.1 = f32[24,128]{1,0:T(8,128)} custom-call(f32[24,128]{1,0:T(8,128)} %pad_bitcast_fusion.v_ref), custom_call_target="tpu_custom_call" | custom-call | tf_op jit(solution)/shard_map/small_sum/pallas_call | solution.py:384
  475.6 1.2 slice.16
  478.1 1.3 slice_bitcast_fusion
  (23 shorter events, 0.2 us)
Async XLA Ops:
  138.0 10.8 %copy-start.2 = (bf16[16,1,128,2048]{3,2,1,0:T(8,128)(2,1)S(1)}, bf16[16,1,128,2048]{3,2,1,0:T(8,128)(2,1)}, u32[]{:S(2)}) copy-start(bf16[16,1,128,2048]{3,2,1,0:T(8,128)(2,1)} %fusion.7) | copy-start | bytes 25165828
  148.6 30.8 %copy-start.1 = (bf16[8,392,2048]{2,1,0:T(8,128)(2,1)}, bf16[8,392,2048]{2,1,0:T(8,128)(2,1)S(1)}, u32[]{:S(2)}) copy-start(bf16[8,392,2048]{2,1,0:T(8,128)(2,1)S(1)} %convert_element_type.31) | copy-start | bytes 38535172
  208.8 20.4 %copy-start = (f32[2048,3136]{0,1:T(8,128)S(1)}, f32[2048,3136]{0,1:T(8,128)}, u32[]{:S(2)}) copy-start(f32[2048,3136]{0,1:T(8,128)} %get-tuple-element.21) | copy-start | bytes 77070336
  208.8 20.4 %copy-start.3 = (f32[16,128]{1,0:T(8,128)S(1)}, f32[16,128]{1,0:T(8,128)}, u32[]{:S(2)}) copy-start(f32[16,128]{1,0:T(8,128)} %get-tuple-element.8) | copy-start | bytes 24580
  238.4 63.3 %slice-start = ((s8[12845056]{0:T(1024)(128)(4,1)}), s8[262144]{0:T(1024)(128)(4,1)S(1)}, s32[]{:S(2)}) async-start(s8[12845056]{0:T(1024)(128)(4,1)} %bitcast.41), calls=%async_computation | async-start | bytes 524288
  265.4 36.4 %slice-start.1 = ((s8[12845056]{0:T(1024)(128)(4,1)}), s8[4194304]{0:T(1024)(128)(4,1)S(1)}, s32[]{:S(2)}) async-start(s8[12845056]{0:T(1024)(128)(4,1)} %bitcast.41), calls=%async_computation.1 | async-start | bytes 8388608
  265.4 36.4 %slice-start.2 = ((s8[12845056]{0:T(1024)(128)(4,1)}), s8[4194304]{0:T(1024)(128)(4,1)S(1)}, s32[]{:S(2)}) async-start(s8[12845056]{0:T(1024)(128)(4,1)} %bitcast.41), calls=%async_computation.2 | async-start | bytes 8388608
  265.4 36.4 %slice-start.3 = ((s8[12845056]{0:T(1024)(128)(4,1)}), s8[4194304]{0:T(1024)(128)(4,1)S(1)}, s32[]{:S(2)}) async-start(s8[12845056]{0:T(1024)(128)(4,1)} %bitcast.41), calls=%async_computation.3 | async-start | bytes 8388608

commit v2 on v0

v2 whole, which is shorter than its diff:
```python
import functools

import jax
import jax.numpy as jnp
from jax import lax
from jax.experimental import pallas as pl
from jax.experimental.pallas import tpu as pltpu
from jax.sharding import PartitionSpec as P

VOCAB_REAL = 49155
LOGIT_SCALE = 6.0
NORM_EPS = 1e-6

AXIS = "vp"
MESH = pl.DeviceIdType.MESH
F32 = jnp.float32
BF16 = jnp.bfloat16
HBM = pltpu.HBM
VMEM = pltpu.VMEM
DMA = pltpu.SemaphoreType.DMA


def _coords():
    me = lax.axis_index(AXIS)
    return me // 32, (me // 8) % 4, (me // 2) % 4, me % 2


def _dev(z, y, x, c):
    return ((z * 4 + y) * 4 + x) * 2 + c


def _mod4(v):
    return lax.rem(v + 8, 4)


def _barrier(peers):
    sem = pltpu.get_barrier_semaphore()
    for p in peers:
        pl.semaphore_signal(sem, inc=1, device_id=(p,), device_id_type=MESH)
    pl.semaphore_wait(sem, len(peers))


def _remote(src, dst, send, recv, k, dev):
    return pltpu.make_async_remote_copy(
        src_ref=src,
        dst_ref=dst,
        send_sem=send.at[k],
        recv_sem=recv.at[k],
        device_id=(dev,),
        device_id_type=MESH,
    )


class Dims:
    def __init__(self, tokens, dim, rows, group):
        self.dim, self.rows = dim, rows
        unit = 128 if rows >= 128 else 64
        self.rm = rows // unit * unit
        self.ha = self.rm // 2
        self.pad = self.rm + 8
        self.chunk = tokens // group
        self.tok = 16 * self.chunk
        self.nt = 2 * self.chunk
        self.main = 8 * self.rm
        self.wide = self.main + 128
        self.h = dim // 2


def _loop_rows(rows, step, fn):
    @pl.loop(0, rows // step)
    def _(i):
        fn(pl.ds(pl.multiple_of(i * step, step), step))


def _fwd_kernel(
    dm, x4, e_ref, g_ref, lab, msk,
    eg, zh, zeh, hh, et, lse_o, pos_o, w_o,
    hv, xst, est, ebf, oext, ext, extb, etst, zst, st, got,
    send, recv, ssend, srecv, esem, xsem, zsem, tsem, hsem,
):
    z, y, x, c = _coords()
    xc, zy = x * 2 + c, z * 4 + y
    rows, rm, ha, dim, chunk, tok, nt = dm.rows, dm.rm, dm.ha, dm.dim, dm.chunk, dm.tok, dm.nt
    right, left = _dev(z, y, _mod4(x + 1), c), _dev(z, y, _mod4(x - 1), c)
    sib = _dev(z, y, x, 1 - c)
    peers = [_dev(_mod4(z + a), _mod4(y + b), x, c) for a in range(4) for b in range(4) if a or b]
    bar = pltpu.get_barrier_semaphore()
    for p in (right, left, sib, *peers):
        pl.semaphore_signal(bar, inc=1, device_id=(p,), device_id_type=MESH)

    def xload(k):
        return pltpu.make_async_copy(x4.at[k, xc], xst.at[lax.rem(k, 2)], xsem.at[lax.rem(k, 2)])

    xload(0).start()

    own = xc
    for j in range(2):
        def widen(r, j=j):
            est[0, j, r, :] = e_ref[pl.ds(j * ha + r.start, r.size), :].astype(F32)

        _loop_rows(ha, 16, widen)
    oext[...] = jnp.zeros_like(oext)
    oext[0 : rows - rm, :] = e_ref[rm:rows, :].astype(F32)
    cps = [pltpu.make_async_copy(est.at[0, j], eg.at[own, pl.ds(j * ha, ha)], esem.at[j]) for j in range(2)]
    cps.append(pltpu.make_async_copy(oext, eg.at[own, pl.ds(rm, 8)], esem.at[2]))
    for cp in cps:
        cp.start()
    for cp in cps:
        cp.wait()
    pl.semaphore_wait(bar, 18)

    a, b = pl.ds(0, ha), pl.ds(ha, ha + 8)

    def piece(s, half, k, dev):
        ref = eg.at[s, half]
        return _remote(ref, ref, send, recv, k, dev)

    def slot(xx):
        return _mod4(xx) * 2 + c

    r_a, r_b = piece(own, a, 0, right), piece(own, b, 1, right)
    l_b, l_a = piece(own, b, 2, left), piece(own, a, 3, left)
    s_o = _remote(eg.at[own], eg.at[own], send, recv, 6, sib)
    for cp in (r_a, l_b, s_o, r_b, l_a):
        cp.start()

    gain = g_ref[...]

    @pl.loop(0, 16)
    def _(k):
        @pl.when(k < 15)
        def _():
            xload(k + 1).start()

        xload(k).wait()

        def norm(r):
            v = xst[lax.rem(k, 2), r, :].astype(F32)
            inv = lax.rsqrt(jnp.mean(v * v, axis=-1, keepdims=True) + NORM_EPS)
            at = pl.multiple_of(k * chunk + r.start, r.size)
            hv[pl.ds(at, r.size), :] = (v * inv * gain).astype(BF16)

        _loop_rows(chunk, 16, norm)

    hout = pltpu.make_async_copy(hv, hh, hsem.at[0])
    hout.start()

    total = jnp.sum(msk[...])
    for k in range(16):
        at = pl.ds(k * chunk, chunk)
        w_o[:, at] = msk[k, xc] / total
        q = lab[k, xc] - zy * (8 * rows)
        s = jnp.zeros_like(q)
        for i in range(1, 8):
            s = s + jnp.where(q >= i * rows, 1, 0)
        r = q - s * rows
        hi = jnp.where(r >= ha, 1, 0)
        at_main = ((s // 2 * 2 + hi) * 2 + s % 2) * ha + r - hi * ha
        at_ext = 8 * rm + s * 8 + r - rm
        place = jnp.where(r < rm, at_main, at_ext)
        pos_o[:, at] = jnp.where((q >= 0) & (q < 8 * rows), place, -1)
    st[0:1, :] = jnp.full((1, tok), -1e30, F32)
    st[1:2, :] = jnp.zeros((1, tok), F32)

    def load(i, xx, half):
        return [
            pltpu.make_async_copy(eg.at[xx * 2 + j, pl.ds(half * ha, ha)], est.at[i, j], esem.at[i * 2 + j])
            for j in range(2)
        ]

    def add_stats(v, lanes):
        m_old, s_old = st[0:1, lanes], st[1:2, lanes]
        m = jnp.maximum(m_old, jnp.max(v, axis=0, keepdims=True))
        s = jnp.sum(jnp.exp(v - m), axis=0, keepdims=True)
        st[0:1, lanes] = m
        st[1:2, lanes] = s_old * jnp.exp(m_old - m) + s

    def product(lhs, lanes):
        v = lax.dot_general(lhs, hv[lanes, :], (((1,), (1,)), ((), ())), preferred_element_type=F32)
        return v * (1.0 / LOGIT_SCALE)

    def logits(i, xx, half):
        first = VOCAB_REAL - ((zy * 8 + xx * 2) * rows + half * ha)
        base = pl.multiple_of((xx * 2 + half) * rm, rm)

        def out(t, s):
            lanes = pl.ds(pl.multiple_of(t * nt, nt), nt)
            return pltpu.make_async_copy(zst.at[s], zh.at[pl.ds(base, rm), lanes], zsem.at[s])

        @pl.loop(0, tok // nt)
        def _(t):
            s = lax.rem(t, 2)

            @pl.when(t >= 2)
            def _():
                out(t, s).wait()

            lanes = pl.ds(pl.multiple_of(t * nt, nt), nt)
            v = product(ebf[i], lanes)
            row = lax.broadcasted_iota(jnp.int32, v.shape, 0)
            lim = jnp.where(row < ha, first, first - rows + ha)
            v = jnp.where(row < lim, v, -jnp.inf)
            zst[s] = v
            out(t, s).start()
            add_stats(v, lanes)

        for s in range(2):
            out(s, s).wait()

    def pair(blocks):
        for i, (xx, half) in enumerate(blocks):
            for cp in load(i, xx, half):
                cp.start()

        @pl.loop(0, 2)
        def _(i):
            xx = jnp.where(i == 0, blocks[0][0], blocks[1][0])
            half = jnp.where(i == 0, blocks[0][1], blocks[1][1])
            for cp in load(i, xx, half):
                cp.wait()
            for j in range(2):
                def narrow(r, j=j):
                    at = pl.multiple_of(j * ha + r.start, r.size)
                    ebf[i, pl.ds(at, r.size), :] = est[i, j, r, :].astype(BF16)

                _loop_rows(ha, 16, narrow)
            logits(i, xx, half)

    def turn(blocks):
        @pl.loop(0, 2)
        def _(i):
            xx = jnp.where(i == 0, blocks[0][0], blocks[1][0])
            half = jnp.where(i == 0, blocks[0][1], blocks[1][1])

            @pl.loop(0, dim // 128)
            def _(d):
                at = pl.ds(pl.multiple_of(d * 128, 128), 128)
                etst[at, 0:rm] = ebf[i, :, at].T

            lanes = pl.ds(pl.multiple_of((xx * 2 + half) * rm, rm), rm)
            cp = pltpu.make_async_copy(etst.at[:, pl.ds(0, rm)], et.at[:, lanes], tsem.at[0])
            cp.start()
            cp.wait()

    xl, xr, xf = _mod4(x - 1), _mod4(x + 1), _mod4(x + 2)
    sl, sr, sf = slot(x - 1), slot(x + 1), slot(x + 2)
    s_o.wait_recv()
    mine = ((x, 0), (x, 1))
    pair(mine)
    turn(mine)

    def ahead(s, half, k, dev):
        cp = piece(s, half, k, dev)
        cp.start()
        return cp

    r_a.wait_recv()
    r_f = ahead(sl, a, 4, right)
    d0 = ahead(sl, a, 7, sib)
    l_b.wait_recv()
    l_f = ahead(sr, b, 5, left)
    d1 = ahead(sr, b, 8, sib)
    d0.wait_recv()
    d1.wait_recv()
    near = ((xl, 0), (xr, 1))
    pair(near)
    turn(near)
    r_b.wait_recv()
    d2 = ahead(sl, b, 9, sib)
    l_a.wait_recv()
    d3 = ahead(sr, a, 10, sib)
    d2.wait_recv()
    d3.wait_recv()
    near = ((xl, 1), (xr, 0))
    pair(near)
    turn(near)
    r_f.wait_recv()
    d4 = ahead(sf, a, 11, sib)
    l_f.wait_recv()
    d5 = ahead(sf, b, 12, sib)
    d4.wait_recv()
    d5.wait_recv()
    ext_loads = [
        pltpu.make_async_copy(eg.at[s, pl.ds(rm, 8)], ext.at[pl.ds(s * 8, 8)], hsem.at[1 + s]) for s in range(8)
    ]
    for cp in ext_loads:
        cp.start()
    far = ((xf, 0), (xf, 1))
    pair(far)
    for cp in ext_loads:
        cp.wait()
    extb[0:64, :] = ext[...].astype(BF16)
    extb[64:128, :] = jnp.zeros((64, dim), BF16)

    @pl.loop(0, tok // nt)
    def _(t):
        lanes = pl.ds(pl.multiple_of(t * nt, nt), nt)
        v = product(extb[0:64, :], lanes)
        row = lax.broadcasted_iota(jnp.int32, v.shape, 0)
        ok = ((row & 7) < rows - rm) & ((zy * 8 + (row >> 3)) * rows + rm + (row & 7) < VOCAB_REAL)
        v = jnp.where(ok, v, -jnp.inf)
        zst[0, 0:64, :] = v
        cp = pltpu.make_async_copy(zst.at[0, pl.ds(0, 64)], zeh.at[:, lanes], zsem.at[0])
        cp.start()
        add_stats(v, lanes)
        cp.wait()

    scps = [_remote(st, got.at[k], ssend, srecv, k, p) for k, p in enumerate(peers)]
    for cp in scps:
        cp.start()
    turn(far)

    @pl.loop(0, dim // 128)
    def _(d):
        at = pl.ds(pl.multiple_of(d * 128, 128), 128)
        etst[at, 0:128] = extb[:, at].T

    ext_out = pltpu.make_async_copy(etst.at[:, pl.ds(0, 128)], et.at[:, pl.ds(dm.main, 128)], tsem.at[0])
    ext_out.start()
    for cp in scps:
        cp.wait_recv()
    m = st[0:1, :]
    top = m
    for k in range(15):
        top = jnp.maximum(top, got[k, 0:1, :])
    s = st[1:2, :] * jnp.exp(m - top)
    for k in range(15):
        s = s + got[k, 1:2, :] * jnp.exp(got[k, 0:1, :] - top)
    lse_o[...] = top + jnp.log(s)
    ext_out.wait()
    hout.wait()
    for cp in (r_a, r_b, l_b, l_a, s_o, r_f, l_f, d0, d1, d2, d3, d4, d5, *scps):
        cp.wait_send()


def _forward(dm, x4, table, gain, labels, mask):
    hbm, vm = pl.BlockSpec(memory_space=HBM), pl.BlockSpec(memory_space=VMEM)
    sd = jax.ShapeDtypeStruct
    d, tok = dm.dim, dm.tok
    return pl.pallas_call(
        functools.partial(_fwd_kernel, dm),
        name="forward",
        out_shape=(
            sd((8, dm.pad, d), F32), sd((dm.main, tok), F32), sd((64, tok), F32), sd((tok, d), BF16),
            sd((d, dm.wide), BF16), sd((1, tok), F32), sd((1, tok), jnp.int32), sd((1, tok), F32),
        ),
        in_specs=[hbm, vm, vm, vm, vm],
        out_specs=(hbm, hbm, hbm, hbm, hbm, vm, vm, vm),
        scratch_shapes=[
            VMEM((tok, d), BF16), VMEM((2, dm.chunk, d), BF16), VMEM((2, 2, dm.ha, d), F32), VMEM((2, dm.rm, d), BF16),
            VMEM((8, d), F32), VMEM((64, d), F32), VMEM((128, d), BF16), VMEM((d, max(dm.rm, 128)), BF16),
            VMEM((2, dm.rm, dm.nt), F32), VMEM((2, tok), F32), VMEM((15, 2, tok), F32),
            DMA((13,)), DMA((13,)), DMA((15,)), DMA((15,)), DMA((4,)), DMA((2,)), DMA((2,)), DMA((1,)), DMA((9,)),
        ],
        compiler_params=pltpu.CompilerParams(
            collective_id=0, has_side_effects=True, vmem_limit_bytes=67043328
        ),
    )(x4, table, gain, labels, mask)


def _bwd_kernel(
    dm, zh, zeh, hh, et, lse, pos, w,
    dh_out, tgt_out, s_h, q_h, xa, xb, xl, xr, dhp, yr,
    hv, etv, dz, zst, od, sst, dee, dht, ya, yb, yl, za, zb, zl, zr, tst,
    send_e, recv_e, send_h, recv_h, bsem, zsem, dsem, osem, hsem, tsem,
):
    z, y, x, c = _coords()
    rm, ha, dim, chunk, tok, h = dm.rm, dm.ha, dm.dim, dm.chunk, dm.tok, dm.h
    hc = h // 2
    xp, xm = _dev(z, y, _mod4(x + 1), c), _dev(z, y, _mod4(x - 1), c)
    yp, ym = _dev(z, _mod4(y + 1), x, c), _dev(z, _mod4(y - 1), x, c)
    zp, zm = _dev(_mod4(z + 1), y, x, c), _dev(_mod4(z - 1), y, x, c)
    sib = _dev(z, y, x, 1 - c)
    peers = (xp, xm, yp, ym, zp, zm, sib)
    bar = pltpu.get_barrier_semaphore()
    for p in peers:
        pl.semaphore_signal(bar, inc=1, device_id=(p,), device_id_type=MESH)
    x_far, x_p, x_m = _mod4(x + 2), _mod4(x + 1), _mod4(x - 1)
    sent = []

    def go(cp):
        cp.start()
        sent.append(cp)
        return cp

    rc = min(64, rm)
    ln = min(512, tok)

    def zload(first, i):
        at = pl.multiple_of(lax.rem(first + i * rc, dm.main), rc)
        s = lax.rem(i, 2)
        return pltpu.make_async_copy(zh.at[pl.ds(at, rc)], zst.at[s], zsem.at[s])

    def dz_tile(s, n, place, store):
        for l in range(tok // ln):
            lanes = pl.ds(l * ln, ln)
            v = zst[s, 0:n, lanes]
            row = lax.broadcasted_iota(jnp.int32, v.shape, 0) + place
            hit = row == pos[:, lanes]
            tgt_out[:, lanes] += jnp.sum(jnp.where(hit, v, 0.0), axis=0, keepdims=True)
            p = jnp.exp(v - lse[:, lanes])
            dz[store, lanes] = (jnp.where(hit, p - 1.0, p) * w[:, lanes]).astype(BF16)

    def dz_rows(first, n):
        @pl.loop(0, n)
        def _(i):
            @pl.when(i + 1 < n)
            def _():
                zload(first, i + 1).start()

            zload(first, i).wait()
            at = pl.multiple_of(lax.rem(first + i * rc, dm.main), rc)
            dz_tile(lax.rem(i, 2), rc, at, pl.ds(at, rc))

    zload(x_far * 2 * rm, 0).start()
    big = [pltpu.make_async_copy(hh, hv, bsem.at[0]), pltpu.make_async_copy(et, etv, bsem.at[1])]
    for cp in big:
        cp.start()
    tgt_out[...] = jnp.zeros_like(tgt_out)
    dz_rows(x_far * 2 * rm, 2 * rm // rc)
    cp = pltpu.make_async_copy(zeh, zst.at[0, pl.ds(0, 64)] if rc >= 64 else zst.at[0], zsem.at[0])
    cp.start()
    cp.wait()
    dz_tile(0, 64, dm.main, pl.ds(dm.main, 64))
    dz[dm.main + 64 : dm.wide, :] = jnp.zeros((64, tok), BF16)
    big[0].wait()

    nd = min(256, dim)

    @pl.loop(0, dim // nd)
    def _(i):
        lanes = pl.ds(pl.multiple_of(i * nd, nd), nd)
        dee[:, lanes] = jnp.dot(dz[dm.main : dm.main + 64, :], hv[:, lanes], preferred_element_type=F32)

    pl.semaphore_wait(bar, len(peers))
    counts = {"d": 0}

    def de_block(xx, half, s):
        at = pl.ds(pl.multiple_of((xx * 2 + half) * rm, rm), rm)

        @pl.loop(0, dim // nd)
        def _(i):
            lanes = pl.ds(pl.multiple_of(i * nd, nd), nd)
            v = jnp.dot(dz[at, :], hv[:, lanes], preferred_element_type=F32)
            od[s, 0, 0:ha, lanes] = v[0:ha]
            od[s, 1, 0:ha, lanes] = v[ha:rm]

        n = ha + 8 * half
        if half:
            for j in range(2):
                od[s, j, ha : ha + 8, :] = dee[pl.ds(pl.multiple_of((xx * 2 + j) * 8, 8), 8), :]
        k = counts["d"]
        counts["d"] += 1
        there = pl.ds(half * ha, n)
        cp = _remote(od.at[s, 1 - c, pl.ds(0, n)], s_h.at[xx, there], send_e, recv_e, k, sib)
        cp.start()
        return xx, half, s, n, cp

    def de_sum(blk):
        xx, half, s, n, cp = blk
        there = pl.ds(half * ha, n)
        cp.wait_recv()
        ld = pltpu.make_async_copy(s_h.at[xx, there], sst.at[pl.ds(0, n)], dsem.at[0])
        ld.start()
        ld.wait()

        def add(r):
            od[s, c, r, :] = od[s, c, r, :] + sst[r, :]

        _loop_rows(n, 8, add)
        out = pltpu.make_async_copy(od.at[s, c, pl.ds(0, n)], q_h.at[xx, there], dsem.at[1])
        out.start()
        out.wait()
        cp.wait_send()

    rows_a, rows_b = pl.ds(0, ha), pl.ds(ha, ha + 8)
    b0 = de_block(x_far, 0, 0)
    b1 = de_block(x_far, 1, 1)
    zload((x_far + 1) * 2 * rm, 0).start()
    dz_rows((x_far + 1) * 2 * rm, 6 * rm // rc)
    de_sum(b0)
    e0 = go(_remote(q_h.at[x_far, rows_a], xa, send_e, recv_e, 8, xp))
    de_sum(b1)
    e1 = go(_remote(q_h.at[x_far, rows_b], xb, send_e, recv_e, 9, xm))

    big[1].wait()
    mt = min(256, h)

    def dh_group(q, n, where):
        def outs(i, s):
            zz, pr = where(i)
            return [
                pltpu.make_async_copy(dht.at[s, j], dhp.at[zz, pr * 2 + j, pl.ds(q * h, h)], hsem.at[s * 2 + j])
                for j in range(2)
            ]

        @pl.loop(0, n)
        def _(i):
            s = lax.rem(i, 2)

            @pl.when(i >= 2)
            def _():
                for cp in outs(i, s):
                    cp.wait()

            zz, pr = where(i)
            lanes = pl.ds(pl.multiple_of((zz * 4 + pr * 2) * chunk, 2 * chunk), 2 * chunk)

            @pl.loop(0, h // mt)
            def _(m):
                v = jnp.dot(
                    etv[pl.ds(pl.multiple_of(q * h + m * mt, mt), mt), :], dz[:, lanes], preferred_element_type=F32
                )
                at = pl.ds(pl.multiple_of(m * mt, mt), mt)
                dht[s, 0, at, :] = v[:, 0:chunk]
                dht[s, 1, at, :] = v[:, chunk : 2 * chunk]

            for cp in outs(i, s):
                cp.start()

        for s in range(2):
            for cp in outs(s, s):
                cp.wait()

    def part(q, p, lo, n):
        rows = pl.ds(q * h, h)
        if q == 0:
            return dhp.at[pl.ds(lo, n), p, rows]
        return dhp.at[p, pl.ds(lo, n), rows]

    ring1, ring2 = ((yp, ym), (zp, zm)), ((zp, zm), (yp, ym))
    pos1, pos2 = (y, z), (z, y)
    first = [[None] * 6, [None] * 6]

    def send_far(q):
        p, (rt, lt) = pos1[q], ring1[q]
        first[q][0] = go(_remote(part(q, _mod4(p + 2), 0, 2), ya.at[q], send_h, recv_h, (q, 0), rt))
        first[q][1] = go(_remote(part(q, _mod4(p + 2), 2, 2), yb.at[q], send_h, recv_h, (q, 1), lt))

    def send_near(q):
        p, (rt, lt) = pos1[q], ring1[q]
        first[q][2] = go(_remote(part(q, _mod4(p + 1), 2, 2), yl.at[q, pl.ds(2, 2)], send_h, recv_h, (q, 2), rt))
        first[q][3] = go(_remote(part(q, _mod4(p - 1), 0, 2), yr.at[q, pl.ds(0, 2)], send_h, recv_h, (q, 3), lt))

    def add_stream(items):
        def loads(i):
            return [
                pltpu.make_async_copy(src, tst.at[i % 2, j], tsem.at[i % 2, j]) for j, src in enumerate(items[i][1])
            ]

        for cp in loads(0):
            cp.start()
        for i, (dst, srcs) in enumerate(items):
            if i + 1 < len(items):
                for cp in loads(i + 1):
                    cp.start()
            for cp in loads(i):
                cp.wait()

            def add(r, i=i, dst=dst, srcs=srcs):
                v = dst[r, :]
                for j in range(len(srcs)):
                    v = v + tst[i % 2, j, r, :]
                dst[r, :] = v

            _loop_rows(h, min(64, h), add)

    def pass_on(q):
        p, (rt, lt) = pos1[q], ring1[q]
        first[q][0].wait_recv()
        add_stream([(ya.at[q, i], [part(q, _mod4(p + 1), i, 1).at[0]]) for i in range(2)] if q == 1 else
                   [(ya.at[q, i], [part(q, _mod4(p + 1), i, 1).at[0]]) for i in range(2)])
        first[q][4] = go(_remote(ya.at[q], yl.at[q, pl.ds(0, 2)], send_h, recv_h, (q, 4), rt))
        first[q][1].wait_recv()
        add_stream([(yb.at[q, i], [part(q, _mod4(p - 1), 2 + i, 1).at[0]]) for i in range(2)])
        first[q][5] = go(_remote(yb.at[q], yr.at[q, pl.ds(2, 2)], send_h, recv_h, (q, 5), lt))

    lo, hi = pl.ds(0, hc), pl.ds(hc, hc)
    second = [[None] * 6, [None] * 6]

    def second_phase(q):
        for cp in first[q][2:]:
            cp.wait_recv()
        add_stream([(yl.at[q, i], [yr.at[q, i], part(q, pos1[q], i, 1).at[0]]) for i in range(4)])
        r, (rt, lt) = pos2[q], ring2[q]
        second[q][0] = go(_remote(yl.at[q, _mod4(r + 2), lo], za.at[q], send_h, recv_h, (q, 6), rt))
        second[q][1] = go(_remote(yl.at[q, _mod4(r + 2), hi], zb.at[q], send_h, recv_h, (q, 7), lt))
        second[q][2] = go(_remote(yl.at[q, _mod4(r + 1), hi], zl.at[q, hi], send_h, recv_h, (q, 8), rt))
        second[q][3] = go(_remote(yl.at[q, _mod4(r - 1), lo], zr.at[q, lo], send_h, recv_h, (q, 9), lt))

    def second_pass(q):
        r, (rt, lt) = pos2[q], ring2[q]
        second[q][0].wait_recv()
        _add_rows(yl.at[q, _mod4(r + 1), lo], [za.at[q]], min(64, hc))
        second[q][4] = go(_remote(yl.at[q, _mod4(r + 1), lo], zl.at[q, lo], send_h, recv_h, (q, 10), rt))
        second[q][1].wait_recv()
        _add_rows(yl.at[q, _mod4(r - 1), hi], [zb.at[q]], min(64, hc))
        second[q][5] = go(_remote(yl.at[q, _mod4(r - 1), hi], zr.at[q, hi], send_h, recv_h, (q, 11), lt))

    def last(q):
        r = pos2[q]
        for cp in second[q][2:]:
            cp.wait_recv()
        _add_rows(yl.at[q, r], [zl.at[q], zr.at[q]], min(64, h))
        cp = pltpu.make_async_copy(yl.at[q, r], dh_out.at[pl.ds(q * h, h)], osem.at[q])
        cp.start()
        return cp

    def ring_sum(xx, rows, n, src, s, k, dst, dev):
        lds = [
            pltpu.make_async_copy(q_h.at[xx, rows], od.at[s, 0, pl.ds(0, n)], dsem.at[0]),
            pltpu.make_async_copy(src, sst.at[pl.ds(0, n)], dsem.at[1]),
        ]
        for cp in lds:
            cp.start()
        for cp in lds:
            cp.wait()

        def add(r):
            od[s, 0, r, :] = od[s, 0, r, :] + sst[r, :]

        _loop_rows(n, 8, add)
        out = pltpu.make_async_copy(od.at[s, 0, pl.ds(0, n)], q_h.at[xx, rows], dsem.at[0])
        out.start()
        out.wait()
        return go(_remote(q_h.at[xx, rows], dst, send_e, recv_e, k, dev))

    pf = _mod4(y + 2) // 2
    dh_group(1, 2, lambda i: (_mod4(z + 2), i))
    send_far(1)
    dh_group(0, 4, lambda i: (i, pf))
    send_far(0)
    dh_group(1, 4, lambda i: (_mod4(z + 1 + 2 * lax.rem(i, 2)), (i < 1) * 1 + (i > 2) * 1))
    send_near(1)
    dh_group(0, 4, lambda i: (i, 1 - pf))
    send_near(0)
    b2 = de_block(x_p, 1, 0)
    b3 = de_block(x_m, 0, 1)
    pass_on(1)
    de_sum(b2)
    e2 = go(_remote(q_h.at[x_p, rows_b], xl.at[rows_b], send_e, recv_e, 10, xp))
    de_sum(b3)
    e3 = go(_remote(q_h.at[x_m, rows_a], xr.at[rows_a], send_e, recv_e, 11, xm))
    pass_on(0)
    dh_group(1, 2, lambda i: (z, i))
    b4 = de_block(x_p, 0, 0)
    b5 = de_block(x_m, 1, 1)
    de_sum(b4)
    e0.wait_recv()
    e4 = ring_sum(x_p, rows_a, ha, xa, 0, 12, xl.at[rows_a], xp)
    de_sum(b5)
    e1.wait_recv()
    e5 = ring_sum(x_m, rows_b, ha + 8, xb, 1, 13, xr.at[rows_b], xm)
    b6 = de_block(x, 0, 0)
    b7 = de_block(x, 1, 1)
    de_sum(b6)
    de_sum(b7)
    second_phase(1)
    second_phase(0)
    second_pass(1)
    second_pass(0)
    outs = [last(1), last(0)]
    for cp in (e2, e3, e4, e5):
        cp.wait_recv()
    for cp in outs:
        cp.wait()
    for cp in sent:
        cp.wait_send()


def _add_rows(dst, srcs, step):
    def add(r):
        acc = dst[r, :]
        for s in srcs:
            acc = acc + s[r, :]
        dst[r, :] = acc

    _loop_rows(dst.shape[0], step, add)


def _backward(dm, zh, zeh, hh, et, lse, pos, w):
    hbm, vm = pl.BlockSpec(memory_space=HBM), pl.BlockSpec(memory_space=VMEM)
    sd = jax.ShapeDtypeStruct
    d, tok, h, ck = dm.dim, dm.tok, dm.h, dm.chunk
    out = pl.pallas_call(
        functools.partial(_bwd_kernel, dm),
        name="backward",
        out_shape=(
            sd((d, ck), F32), sd((1, tok), F32), sd((4, dm.pad, d), F32), sd((4, dm.pad, d), F32),
            sd((dm.ha, d), F32), sd((dm.ha + 8, d), F32), sd((dm.pad, d), F32), sd((dm.pad, d), F32),
            sd((4, 4, d, ck), F32), sd((2, 4, h, ck), F32),
        ),
        in_specs=[hbm, hbm, hbm, hbm, vm, vm, vm],
        out_specs=(hbm, vm, hbm, hbm, hbm, hbm, hbm, hbm, hbm, hbm),
        scratch_shapes=[
            VMEM((tok, d), BF16), VMEM((d, dm.wide), BF16), VMEM((dm.wide, tok), BF16), VMEM((2, 64, tok), F32),
            VMEM((2, 2, dm.ha + 8, d), F32), VMEM((dm.ha + 8, d), F32), VMEM((64, d), F32), VMEM((2, 2, h, ck), F32),
            VMEM((2, 2, h, ck), F32), VMEM((2, 2, h, ck), F32), VMEM((2, 4, h, ck), F32),
            VMEM((2, h // 2, ck), F32), VMEM((2, h // 2, ck), F32), VMEM((2, h, ck), F32), VMEM((2, h, ck), F32),
            VMEM((2, 2, h, ck), F32),
            DMA((14,)), DMA((14,)), DMA((2, 12)), DMA((2, 12)), DMA((2,)), DMA((2,)), DMA((2,)), DMA((2,)),
            DMA((4,)), DMA((2, 2)),
        ],
        compiler_params=pltpu.CompilerParams(
            collective_id=1, has_side_effects=True, vmem_limit_bytes=67043328
        ),
    )(zh, zeh, hh, et, lse, pos, w)
    dh_t, tgt, _, q_h, _, _, xl, xr, _, _ = out
    return dh_t, tgt, q_h, xl, xr


def _allsum_kernel(v_ref, o_ref, mid, got1, got2, send1, recv1, send2, recv2):
    z, y, x, c = _coords()
    near = [_dev(_mod4(z + a), _mod4(y + b), x, c) for a in range(4) for b in range(4) if a or b]
    far = [_dev(z, y, _mod4(x + a), lax.rem(c + b, 2)) for a in range(4) for b in range(2) if a or b]
    _barrier(near + far)
    cps = [_remote(v_ref, got1.at[k], send1, recv1, k, dev) for k, dev in enumerate(near)]
    for cp in cps:
        cp.start()
    for cp in cps:
        cp.wait_recv()
    tot = v_ref[...]
    for k in range(15):
        tot = tot + got1[k]
    mid[...] = tot
    cps2 = [_remote(mid, got2.at[k], send2, recv2, k, dev) for k, dev in enumerate(far)]
    for cp in cps2:
        cp.start()
    for cp in cps2:
        cp.wait_recv()
    tot = mid[...]
    for k in range(7):
        tot = tot + got2[k]
    o_ref[...] = tot
    for cp in cps + cps2:
        cp.wait_send()


def _allsum(v):
    vm = pl.BlockSpec(memory_space=VMEM)
    return pl.pallas_call(
        _allsum_kernel,
        name="small_sum",
        out_shape=jax.ShapeDtypeStruct(v.shape, F32),
        in_specs=[vm],
        out_specs=vm,
        scratch_shapes=[
            VMEM(v.shape, F32), VMEM((15, *v.shape), F32), VMEM((7, *v.shape), F32),
            DMA((15,)), DMA((15,)), DMA((7,)), DMA((7,)),
        ],
        compiler_params=pltpu.CompilerParams(collective_id=3, has_side_effects=True),
    )(v)


def solution(mesh):
    group = mesh.shape[AXIS]

    def local_step(residual, labels, loss_mask, norm_gain, table_shard):
        tokens, dim = residual.shape
        rows = table_shard.shape[0]
        dm = Dims(tokens, dim, rows, group)
        chunk = dm.chunk
        me = lax.axis_index(AXIS)
        x4 = residual.reshape(16, 8, chunk, dim)
        lab = labels.reshape(16, 8, 1, chunk)
        msk = loss_mask.reshape(16, 8, 1, chunk)
        _, zh, zeh, hh, et, lse, pos, w = _forward(dm, x4, table_shard, norm_gain[None, :], lab, msk)
        dh_t, tgt, q_h, xl, xr = _backward(dm, zh, zeh, hh, et, lse, pos, w)

        own = lax.dynamic_index_in_dim(q_h, (me // 2) % 4, 0, keepdims=False)
        d_embed = (own + xl + xr)[:rows] / LOGIT_SCALE
        dh = dh_t.T / LOGIT_SCALE
        x_loc = lax.dynamic_slice_in_dim(residual, me * chunk, chunk, axis=0).astype(F32)
        inv_loc = lax.rsqrt(jnp.mean(x_loc * x_loc, axis=-1, keepdims=True) + NORM_EPS)
        x_hat = x_loc * inv_loc
        dg_part = jnp.sum(dh * x_hat, axis=0)
        loss_part = jnp.sum(w * (jnp.where(me // 8 == 0, lse, 0.0) - tgt))
        small = jnp.concatenate([dg_part, jnp.full((1024,), loss_part)]).reshape(-1, 128)
        small = _allsum(small).reshape(-1)
        u = dh * norm_gain
        d_res = inv_loc * (u - x_hat * jnp.mean(u * x_hat, axis=-1, keepdims=True))
        return small[dim], d_res, d_embed, small[:dim]

    return jax.shard_map(
        local_step,
        mesh=mesh,
        in_specs=(P(), P(), P(), P(), P(AXIS, None)),
        out_specs=(P(), P(AXIS, None), P(AXIS, None), P()),
        check_vma=False,
    )
```

time: 1380 us -> 371 us (0.27)
  waiting for transfers between devices: 1040 us -> 0 us
  Pallas kernels: 0 us -> 354 us
  matrix products: 140 us -> 0 us
  other arithmetic: 107 us -> 4.56 us
  blocking collectives: 68.2 us -> 0 us
  between operations: 16.3 us -> 0.8 us
    unnamed x4 -> x0, waiting for transfers between devices: 747 us -> none
    pallas_call x0 -> x3, Pallas kernels: none -> 354 us  [the longest x1 187 us: _backward(): pl.pallas_call(functools.partial(_bwd_kernel, dm), name='backward', out_s...]
    pmax x1 -> x0, waiting for transfers between devices: 149 us -> none  [local_step(): row_max = lax.pmax(jnp.max(logits, axis=-1), vp_axis)]
    psum x1 -> x0, waiting for transfers between devices: 145 us -> none  [local_step(): row_stats = lax.psum(part_stats, vp_axis)]
    dot_general x3 -> x0, matrix products: 140 us -> none  [the longest x1 58.7 us: local_step(): jnp.dot(d_logits, table_shard, preferred_element_type=jnp.float32)]
    mul x2, other arithmetic: 68.9 us -> 0.34 us  [the longest x1 0.34 us: local_step(): d_res = inv_loc * (u - x_hat * jnp.mean(u * x_hat, axis=-1, keepdims=True))]
    psum x1 -> x0, blocking collectives: 68.2 us -> none  [local_step(): d_gain = lax.psum(jnp.sum(d_hidden * x_hat_loc, axis=0), vp_axis)]
    reduce_sum x4 -> x3, other arithmetic: 36.9 us -> 1.54 us  [the longest x1 0.63 us: local_step(): d_res = inv_loc * (u - x_hat * jnp.mean(u * x_hat, axis=-1, keepdims=True))]
  transfers between devices with their start and end apart: 3 -> 0, of which waited for: 3 -> 0; matrix products, arithmetic and copies ran while one was open for 8% -> 0% of each run, Pallas kernels for 0% -> 0%
where the time goes in v2:
time: 371 us; the launch traced here: 370 us
  Pallas kernels  354 us (95%)
  local copies, waits for them, and re-layouts  10.3 us (3%)
  other arithmetic  4.56 us (1%)
    pallas_call x1, Pallas kernels, _backward(): pl.pallas_call(functools.partial(_bwd_kernel, dm), name='backward', out_s...  187 us
    pallas_call x1, Pallas kernels, _forward(): pl.pallas_call(functools.partial(_fwd_kernel, dm), name='forward', out_sh...  153 us
    pallas_call x1, Pallas kernels, _allsum(): pl.pallas_call(_allsum_kernel, name='small_sum', out_shape=jax.ShapeDtype...  13.9 us

profile of v2, /device:TPU:1, one launch (start us, length us, event | category | flops | bytes accessed | tf_op | source)
XLA Modules:
  0.0 369.6 jit_solution(15625747397928522866)
XLA Ops:
  0.7 153.2 %forward.1 = (f32[8,392,2048]{2,1,0:T(8,128)}, f32[3072,2048]{1,0:T(8,128)}, f32[64,2048]{1,0:T(8,128)}, bf16[2048,2048]{1,0:T(8,128)(2,1)}, bf16[2048,3200]{1,0...) custom-call(bf16[16,8,128,2048]{3,2,1,0:T(8,128)(2,1)} %bitcast.x4, ...), custom_call_target="tpu_custom_call" | custom-call | tf_op jit(solution)/shard_map/forward/pallas_call | solution.py:340
  153.9 186.9 %backward.1 = (f32[2048,128]{1,0:T(8,128)}, f32[1,2048]{1,0:T(1,128)}, f32[4,392,2048]{2,1,0:T(8,128)}, f32[4,392,2048]{2,1,0:T(8,128)}, f32[192,2048]{1,0:T(8,1...) custom-call(f32[3072,2048]{1,0:T(8,128)} %get-tuple-element.16.zh, ...), custom_call_target="tpu_custom_call" | custom-call | tf_op jit(solution)/shard_map/backward/pallas_call | solution.py:685
  340.8 0.0 copy-start.1
  340.8 0.0 copy-start.2
  340.8 2.4 dynamic-slice_bitcast_fusion
  343.2 0.4 copy-done.1
  343.7 1.0 copy-done.2
  344.6 0.0 copy-start.5
  344.6 2.7 fusion
  347.3 0.0 copy-start
  347.3 1.2 constant_dynamic-slice_fusion
  348.5 0.3 copy.11
  348.8 0.3 fusion.8
  349.0 0.0 copy-start.3
  349.0 0.0 copy-start.4
  349.1 0.0 copy-start.6
  349.1 0.0 copy-done.5
  349.1 0.0 copy-done
  349.1 0.6 fusion.5
  349.8 0.3 fusion.7
  350.1 1.3 copy.10
  351.4 0.0 copy-done.3
  351.4 0.0 copy-done.4
  351.4 0.0 copy-done.6
  351.4 0.6 fusion.11
  352.0 1.2 pad_bitcast_fusion.v_ref
  353.3 13.9 %small_sum.1 = f32[24,128]{1,0:T(8,128)} custom-call(f32[24,128]{1,0:T(8,128)} %pad_bitcast_fusion.v_ref), custom_call_target="tpu_custom_call" | custom-call | tf_op jit(solution)/shard_map/small_sum/pallas_call | solution.py:741
  367.2 1.3 slice_bitcast_fusion
  368.5 1.2 slice.16
  (3 shorter events, 0.0 us)
Async XLA Ops:
  340.8 2.9 copy-start.1
  340.8 3.8 %copy-start.2 = (f32[392,2048]{1,0:T(8,128)S(1)}, f32[392,2048]{1,0:T(8,128)}, u32[]{:S(2)}) copy-start(f32[392,2048]{1,0:T(8,128)} %get-tuple-element.27) | copy-start | bytes 9633796
  344.6 4.4 %copy-start.5 = (f32[2048]{0:T(1024)S(1)}, f32[2048]{0:T(1024)}, u32[]{:S(2)}) copy-start(f32[2048]{0:T(1024)} %param.8) | copy-start | bytes 24580
  347.3 1.8 copy-start
  349.0 2.4 copy-start.3
  349.0 2.4 copy-start.4
  349.1 2.4 copy-start.6
